TPU v7x, 128 devices: a whole 4x4x4 slice. The times are simulated.
128 devices in a mesh: node: 128 (over x, z, y, core).
Axes of the slice: x: 4, y: 4, z: 4, core: 2. Of those that a mesh axis runs over, the one named last changes fastest.
Arguments:
- event_node: int32 [65536], P('node'), may hold values from 0 to 32767, as said below
- neighbours: int32 [65536, 10], P('node'), may hold values from 0 to 32767, as said below
- event_bucket: int32 [65536], P('node'), may hold values from 0 to 127
- neighbour_bucket: int32 [65536, 10], P('node'), may hold values from 0 to 127
- edge_features: bfloat16 [65536, 128], P('node'), may hold values from -6 to 6
- affinity: float32 [65536, 10], P('node'), may hold values from -320 to 320
- upstream: bfloat16 [65536, 512], P('node'), may hold values from -6 to 6
- node_memory: bfloat16 [32768, 512], P('node'), may hold values from -4 to 4
- edge_weight: bfloat16 [128, 512], replicated, may hold values from -0.5 to 0.5
- time_message: float32 [128, 512], replicated, may hold values from -6 to 6
- input_weight: bfloat16 [512, 1536], replicated, may hold values from -0.25 to 0.25
- hidden_weight: bfloat16 [512, 1536], replicated, may hold values from -0.25 to 0.25
- gate_bias: float32 [1536], replicated, may hold values from -6 to 6
- time_key: float32 [128, 512], replicated, may hold values from -6 to 6
- query_weight: bfloat16 [512, 512], replicated, may hold values from -0.25 to 0.25
- key_weight: bfloat16 [512, 512], replicated, may hold values from -0.25 to 0.25
- value_weight: bfloat16 [512, 512], replicated, may hold values from -0.25 to 0.25
- out_weight: bfloat16 [512, 512], replicated, may hold values from -0.25 to 0.25
Outputs:
- embedding: bfloat16 [65536, 512], P('node')
- new_memory: bfloat16 [32768, 512], P('node')
- grad_query: float32 [512, 512], replicated
- grad_key: float32 [512, 512], replicated
- grad_value: float32 [512, 512], replicated
- grad_out: float32 [512, 512], replicated
Inputs may be any that keep to these rules, and one draw needn't show every extreme that they name: `event_node`: node i belongs to index i // 256 of node. Of the 512 rows of one device, at most 12 name nodes of one index; in every draw one index receives exactly 12 of them from every device. `neighbours`: node i belongs to index i // 256 of node. Of the 5120 entries of one device's rows, at most 80 name nodes of one index, and these name at most 64 distinct nodes; in every draw one index receives exactly 80 entries naming exactly 64 distinct nodes from every device.
All inputs are finite; a program needn't handle non-finite values.
Results may differ from a plain program's by a relative error of at most 0.012.
Values may be sent and summed in bfloat16 or wider, within the bound.
No kernel may reach another device: no remote copies, remote signals or barrier semaphores. Data moves between devices by JAX's collectives and lax.ppermute only.
A program may use at most 192 MiB of HBM per device.

v0:
```python
import math

import jax
import jax.numpy as jnp
from jax import lax
from jax.sharding import PartitionSpec as P

HEADS = 2


def table_rows(table, buckets):
    picks = (buckets[:, None] == jnp.arange(table.shape[0], dtype=jnp.int32)[None, :]).astype(
        jnp.float32
    )
    return jnp.dot(
        picks, table, precision=lax.Precision.HIGHEST, preferred_element_type=jnp.float32
    )


def make_message(edge_rows, buckets, edge_weight, time_message):
    before = jnp.dot(edge_rows, edge_weight, preferred_element_type=jnp.float32) + table_rows(
        time_message, buckets
    )
    return jax.nn.silu(before).astype(jnp.bfloat16)


def place_slots(node_ids, node_rows, devices, capacity):
    amount = node_ids.shape[0]
    owners = node_ids // node_rows
    marked = (owners[:, None] == jnp.arange(devices, dtype=jnp.int32)[None, :]).astype(jnp.int32)
    earlier_marks = jnp.cumsum(marked, axis=0) - marked
    ranking = jnp.sum(earlier_marks * marked, axis=1)
    slot_of = owners * capacity + ranking
    holder = (
        jnp.full((devices * capacity,), amount, jnp.int32)
        .at[slot_of]
        .set(jnp.arange(amount, dtype=jnp.int32))
    )
    return (slot_of, holder)


def gru_rows(aggregate, previous, input_weight, hidden_weight, gate_bias):
    columns = previous.shape[1]
    inputs = jnp.dot(aggregate, input_weight, preferred_element_type=jnp.float32) + gate_bias
    hidden = jnp.dot(previous, hidden_weight, preferred_element_type=jnp.float32)
    update = jax.nn.sigmoid(inputs[:, :columns] + hidden[:, :columns])
    resets = jax.nn.sigmoid(inputs[:, columns : 2 * columns] + hidden[:, columns : 2 * columns])
    candidate = jnp.tanh(inputs[:, 2 * columns :] + resets * hidden[:, 2 * columns :])
    return (1.0 - update) * candidate + update * previous.astype(jnp.float32)


def attend(
    target,
    neighbour_rows,
    neighbour_bucket,
    affinity,
    time_key,
    query_weight,
    key_weight,
    value_weight,
    out_weight,
):
    events, fanout, columns = neighbour_rows.shape
    head_size = columns // HEADS
    query = (
        jnp.dot(target, query_weight, preferred_element_type=jnp.float32)
        .astype(jnp.bfloat16)
        .reshape(events, HEADS, head_size)
    )
    flat_rows = neighbour_rows.reshape(events * fanout, columns)
    key_rows = jnp.dot(flat_rows, key_weight, preferred_element_type=jnp.float32) + table_rows(
        time_key, neighbour_bucket.reshape(-1)
    )
    key_rows = key_rows.astype(jnp.bfloat16).reshape(events, fanout, HEADS, head_size)
    value_rows = (
        jnp.dot(flat_rows, value_weight, preferred_element_type=jnp.float32)
        .astype(jnp.bfloat16)
        .reshape(events, fanout, HEADS, head_size)
    )
    scores = jnp.einsum(
        "ehd,enhd->ehn", query, key_rows, preferred_element_type=jnp.float32
    ) / math.sqrt(head_size)
    scores = scores + affinity[:, None, :]
    probs = jax.nn.softmax(scores, axis=-1).astype(jnp.bfloat16)
    mixed = jnp.einsum("ehn,enhd->ehd", probs, value_rows, preferred_element_type=jnp.float32)
    mixed = mixed.astype(jnp.bfloat16).reshape(events, columns)
    return (
        jnp.dot(mixed, out_weight, preferred_element_type=jnp.float32) + target.astype(jnp.float32)
    ).astype(jnp.bfloat16)


def shards(
    event_node,
    neighbours,
    event_bucket,
    neighbour_bucket,
    edge_features,
    affinity,
    upstream,
    node_memory,
    edge_weight,
    time_message,
    input_weight,
    hidden_weight,
    gate_bias,
    time_key,
    query_weight,
    key_weight,
    value_weight,
    out_weight,
):
    devices = lax.axis_size("node")
    node_rows = node_memory.shape[0]
    columns = node_memory.shape[1]
    events = neighbours.shape[0]
    fanout = neighbours.shape[1]
    cap_message = 3 * events // devices
    slot_event, holder_event = place_slots(event_node, node_rows, devices, cap_message)
    filled = holder_event < events
    source = jnp.minimum(holder_event, events - 1)
    local_target = jnp.where(filled, event_node[source] % node_rows, node_rows).reshape(
        devices, cap_message
    )
    messages = make_message(edge_features, event_bucket, edge_weight, time_message)
    outgoing = jnp.where(filled[:, None], messages[source], jnp.zeros((), jnp.bfloat16)).reshape(
        devices, cap_message, -1
    )
    rows_in, arrived = (
        lax.all_to_all(local_target, "node", split_axis=0, concat_axis=0, tiled=True),
        lax.all_to_all(outgoing, "node", split_axis=0, concat_axis=0, tiled=True),
    )
    arrived = arrived.reshape(devices * cap_message, -1)
    flat_in = rows_in.reshape(-1)
    totals = jax.ops.segment_sum(arrived.astype(jnp.float32), flat_in, num_segments=node_rows + 1)[
        :node_rows
    ]
    counts = jax.ops.segment_sum(
        jnp.ones(flat_in.shape, jnp.float32), flat_in, num_segments=node_rows + 1
    )[:node_rows]
    aggregate = (totals / jnp.maximum(counts, 1.0)[:, None]).astype(jnp.bfloat16)
    updated = gru_rows(aggregate, node_memory, input_weight, hidden_weight, gate_bias)
    new_memory = jnp.where(counts[:, None] > 0, updated, node_memory.astype(jnp.float32)).astype(
        jnp.bfloat16
    )
    padded = jnp.concatenate([new_memory, jnp.zeros((1, columns), jnp.bfloat16)], axis=0)
    returned = lax.all_to_all(
        padded[flat_in].reshape(devices, cap_message, columns),
        "node",
        split_axis=0,
        concat_axis=0,
        tiled=True,
    )
    target = returned.reshape(-1, columns)[slot_event]
    entries = neighbours.reshape(-1)
    whole_table = lax.all_gather(new_memory, "node", axis=0, tiled=True)
    nearby = whole_table[entries].reshape(events, fanout, columns)

    def forward(weight_q, weight_k, weight_v, weight_o):
        return attend(
            target,
            nearby,
            neighbour_bucket,
            affinity,
            time_key,
            weight_q,
            weight_k,
            weight_v,
            weight_o,
        )

    embedding, pullback = jax.vjp(forward, query_weight, key_weight, value_weight, out_weight)
    grad_q, grad_k, grad_v, grad_o = pullback(upstream)
    summed = lax.psum(
        (
            grad_q.astype(jnp.float32),
            grad_k.astype(jnp.float32),
            grad_v.astype(jnp.float32),
            grad_o.astype(jnp.float32),
        ),
        "node",
    )
    factor = 1.0 / math.sqrt(events * devices)
    return (
        embedding,
        new_memory,
        summed[0] * factor,
        summed[1] * factor,
        summed[2] * factor,
        summed[3] * factor,
    )


def solution(mesh):
    placed = (
        P("node"),
        P("node", None),
        P("node"),
        P("node", None),
        P("node", None),
        P("node", None),
        P("node", None),
        P("node", None),
        P(),
        P(),
        P(),
        P(),
        P(),
        P(),
        P(),
        P(),
        P(),
        P(),
    )
    return jax.shard_map(
        shards,
        mesh=mesh,
        in_specs=placed,
        out_specs=(P("node", None), P("node", None), P(), P(), P(), P()),
        check_vma=False,
    )
```

profile of v0, /device:TPU:1, one launch (start us, length us, event | category | flops | bytes accessed | tf_op | source)
XLA Modules:
  0.0 648.8 jit_solution(6930002317344260239)
XLA Ops:
  7.2 0.8 fusion.86
  8.0 0.7 add_select_fusion.1
  9.4 0.7 compare_select_fusion.3
  10.1 2.5 scatter_custom_fusion
  12.6 9.5 %gather_fusion = s32[1536]{0:T(1024)S(1)} fusion(s32[512]{0:T(512)S(1)} %copy-done.2, s32[2048]{0:T(1024)S(1)} %pad_clamp_fusion.1), kind=kCustom, calls=%fused_computation | custom fusion | bytes 18432 | tf_op jit(solution)/shard_map/gather | solution.py:121
  22.1 0.7 all_to_all.12
  22.8 11.5 %all-to-all-start = ((s32[128,1,12]{2,1,0:T(1,128)}), s32[128,1,12]{2,1,0:T(1,128)S(1)}, u32[]{:S(2)}, u32[]{:S(2)}) async-start(s32[128,1,12]{2,1,0:T(1,128)} %bitcast.6), calls=%async_computation | async-start | bytes 131072 | tf_op jit(solution)/shard_map/all_to_all | solution.py:129
  34.5 0.6 fusion.41
  35.1 0.4 multiply_convert_fusion.2
  35.6 5.4 gather_fusion.1
  41.0 3.7 gather.19
  44.7 2.8 broadcast_select_fusion
  47.5 10.2 %all-to-all-start.1 = ((bf16[128,12,512]{2,1,0:T(8,128)(2,1)}), bf16[128,12,512]{2,1,0:T(8,128)(2,1)}, u32[]{:S(2)}, u32[]{:S(2)}) async-start(bf16[128,12,512]{2,1,0:T(8,128)(2,1)} %broadcast_select_fusion), calls=%async_computation.1 | async-start | bytes 4194304 | tf_op jit(solution)/shard_map/all_to_all | solution.py:130
  57.8 0.6 fusion.57
  58.4 0.5 broadcast.161
  58.9 0.8 reduce.11
  59.8 11.1 %scatter_custom_fusion.1 = f32[257]{0:T(512)S(1)} fusion(s32[1536]{0:T(1024)S(1)} %reshape.218, f32[1536]{0:T(1024)S(1)} %broadcast.111, f32[]{:T(128)} %constant.22.clone.1), kind=kCustom, calls=%fused_computation.117 | custom fusion | flops 1536 | bytes 1032 | tf_op jit(solution)/shard_map/scatter-add | solution.py:137
  71.0 16.6 %all-to-all-done.1 = bf16[128,12,512]{2,1,0:T(8,128)(2,1)} async-done(((bf16[128,12,512]{2,1,0:T(8,128)(2,1)}), bf16[128,12,512]{2,1,0:T(8,128)(2,1)}, u32[]{:S(2)}, u32[]{:S(2)}) %all-to-all-start.1) | async-done | bytes 1572896 | tf_op jit(solution)/shard_map/all_to_all | solution.py:130
  87.6 3.9 reshape.228
  91.5 11.2 %scatter_custom_fusion.2 = f32[257,512]{1,0:T(8,128)} fusion(s32[1536]{0:T(1024)S(1)} %reshape.218, f32[1536,512]{1,0:T(8,128)} %reshape.228, f32[]{:T(128)} %constant.22.clone.1), kind=kCustom, calls=%fused_computation.76 | custom fusion | flops 786432 | bytes 526848 | tf_op jit(solution)/shard_map/scatter-add | solution.py:134
  102.7 2.2 convolution_add_fusion
  104.9 1.1 fusion.20
  106.2 1.0 concatenate.3
  107.1 4.8 gather_fusion.2
  112.0 1.6 reshape.156
  113.6 5.9 all-to-all-start.2
  119.5 0.5 convolution_convert_fusion.5
  121.3 29.6 %all-to-all-done.2 = bf16[128,12,512]{2,1,0:T(8,128)(2,1)} async-done(((bf16[128,12,512]{2,1,0:T(8,128)(2,1)}), bf16[128,12,512]{2,1,0:T(8,128)(2,1)}, u32[]{:S(2)}, u32[]{:S(2)}) %all-to-all-start.2) | async-done | bytes 1572896 | tf_op jit(solution)/shard_map/all_to_all | solution.py:146
  150.9 2.6 reshape.157
  153.6 2.0 gather_fusion.3
  155.6 1.5 convolution_convert_fusion.6
  157.1 0.4 copy.59
  157.5 70.5 %all-gather.2.cloned.1.call-done = bf16[32768,512]{1,0:T(8,128)(2,1)} async-done(((bf16[256,512]{1,0:T(8,128)(2,1)}), bf16[32768,512]{1,0:T(8,128)(2,1)}) %all-gather.2.cloned.1.call-update) | async-done | bytes 33554448 | tf_op jit(solution)/shard_map/all_gather | solution.py:155
  228.0 83.5 %gather_fusion.4 = bf16[5120,512]{1,0:T(8,128)(2,1)} fusion(bf16[32768,512]{1,0:T(8,128)(2,1)} %all-gather.2.cloned.1.call-done, s32[5120]{0:T(1024)S(1)} %broadcast_clamp_fusion), kind=kCustom, calls=%fused_computation.4 | custom fusion | bytes 10506240 | tf_op jit(solution)/shard_map/gather | solution.py:156
  311.5 7.1 %convolution_convert_fusion = bf16[5120,512]{1,0:T(8,128)(2,1)} fusion(bf16[5120,512]{1,0:T(8,128)(2,1)} %gather_fusion.4, bf16[512,512]{1,0:T(8,128)(2,1)S(1)} %copy-done.18), kind=kOutput, calls=%fused_computation.18 | convolution fusion | flops 2686976000 | bytes 11010048 | tf_op jit(solution)/shard_map/jvp()/dot_general | solution.py:76
  318.5 8.4 %reshape.161 = bf16[512,10,2,256]{3,2,1,0:T(2,128)(2,1)} reshape(bf16[5120,512]{1,0:T(8,128)(2,1)} %convolution_convert_fusion) | data formatting | bytes 10485760 | tf_op jit(solution)/shard_map/jvp()/reshape | solution.py:78
  326.9 4.9 fusion.58
  331.8 6.8 %add_convert_fusion = bf16[5120,512]{1,0:T(8,128)(2,1)} fusion(f32[5120,512]{1,0:T(8,128)S(1)} %fusion.58, f32[128,512]{1,0:T(8,128)S(1)} %copy-done.12, s32[5120]{0:T(1024)S(1)} %eq.63), kind=kOutput, calls=%fused_computation.13 | convolution fusion | flops 4032430080 | bytes 16011264 | tf_op jit(solution)/shard_map/jvp()/dot_general | solution.py:15
  338.6 8.3 %reshape.160 = bf16[512,10,2,256]{3,2,1,0:T(2,128)(2,1)} reshape(bf16[5120,512]{1,0:T(8,128)(2,1)} %add_convert_fusion) | data formatting | bytes 10485760 | tf_op jit(solution)/shard_map/jvp()/reshape | solution.py:74
  346.9 9.7 %multiply_reduce_fusion.1 = f32[512,2,10]{1,2,0:T(8,128)S(1)} fusion(f32[512,2,256]{2,1,0:T(2,128)S(1)} %copy.59, bf16[512,10,2,256]{3,2,1,0:T(2,128)(2,1)} %reshape.160), kind=kLoop, calls=%fused_computation.10 | loop fusion | flops 7854080 | bytes 6332416 | tf_op jit(solution)/shard_map/jvp(ehd,enhd->ehn)/dot_general | solution.py:80
  356.7 51.3 %fusion.56 = (f32[512,2]{1,0:T(8,128)S(1)}, f32[512,2,10]{1,2,0:T(8,128)S(1)}) fusion(f32[512,2,10]{1,2,0:T(8,128)S(1)} %multiply_reduce_fusion.1, f32[512,10]{1,0:T(8,128)S(1)} %copy.39), kind=kOutput, calls=%fused_computation.124 | output fusion | flops 61449 | bytes 106496 | tf_op jit(solution)/shard_map/jvp()/sub | solution.py:84
  408.1 12.3 %multiply_reduce_fusion = bf16[512,2,10]{1,2,0:T(8,128)(2,1)S(1)} fusion(f32[512,2,256]{2,1,0:T(2,128)S(1)} %copy.60, bf16[512,10,2,256]{3,2,1,0:T(2,128)(2,1)S(1)} %bitcast.79), kind=kLoop, calls=%fused_computation.9 | loop fusion | flops 7854080 | bytes 6311936 | tf_op jit(solution)/shard_map/transpose(jvp(ehn,enhd->ehd))/dot_general | solution.py:85
  420.4 1.5 fusion.9
  422.0 3.5 fusion.54
  425.5 8.2 %multiply_convert_fusion = bf16[512,2,256,10]{2,1,3,0:T(2,128)(2,1)S(1)} fusion(f32[512,2,256]{2,1,0:T(2,128)S(1)} %copy.60, f32[512,2,10]{1,2,0:T(8,128)S(1)} %get-tuple-element.12), kind=kLoop, calls=%fused_computation.11 | loop fusion | flops 5242880 | bytes 6332416 | tf_op jit(solution)/shard_map/transpose(jvp(ehn,enhd->ehd))/convert_element_type | solution.py:85
  433.7 0.9 copy.66
  434.9 3.9 fusion.14
  438.8 8.1 %copy.48 = bf16[512,2,10,1]{2,3,1,0:T(2,128)(2,1)S(1)} copy(bf16[512,2,10,1]{1,2,0,3:T(8,128)(2,1)} %get-tuple-element.14) | data formatting | bytes 40960 | tf_op jit(solution)/shard_map/jvp()/convert_element_type | solution.py:84
  446.9 3.9 fusion.3
  450.8 0.5 copy.74
  451.5 1.4 fusion.17
  453.3 9.1 %multiply_convert_fusion.1 = bf16[512,2,10,256]{3,1,2,0:T(2,128)(2,1)} fusion(f32[512,2,256]{2,1,0:T(2,128)S(1)} %copy.59, f32[512,2,10]{1,2,0:T(8,128)S(1)} %copy-done.3), kind=kLoop, calls=%fused_computation.12 | loop fusion | flops 5242880 | bytes 6332416 | tf_op jit(solution)/shard_map/transpose(jvp(ehd,enhd->ehn))/convert_element_type | solution.py:80
  462.4 8.7 %copy.56 = bf16[512,2,10,1]{2,3,1,0:T(2,128)(2,1)S(1)} copy(f32[512,2,10,1]{1,2,0,3:T(8,128)} %bitcast.73) | data formatting | bytes 61440 | tf_op jit(solution)/shard_map/transpose(jvp())/div | solution.py:80
  471.1 4.0 fusion.1
  475.1 0.5 copy.73
  475.7 1.4 fusion.16
  477.2 0.9 copy.65
  478.2 0.5 slice-done.3
  478.7 3.9 fusion.15
  482.6 1.0 copy-done.7
  483.6 1.2 fusion.18
  484.8 151.9 %all-reduce.4.cloned.1.call-done = (f32[512,512]{1,0:T(8,128)}, f32[512,512]{1,0:T(8,128)}, f32[512,512]{1,0:T(8,128)}, f32[512,512]{1,0:T(8,128)}) async-done(((f32[512,512]{1,0:T(8,128)}, f32[512,512]{1,0:T(8,128)}, f32[512,512]{1,0:T(8,128)}, f32[512,512]{1,0:T(8,128)}), (f32[512,512]{1,0:T(8,128)}, f32[512,512]{1,0:T(8,128)}, f32[512,512]{1,0:T(8,128)}, ...) | async-done | bytes 4194320 | tf_op jit(solution)/shard_map/psum | solution.py:173
  636.7 3.2 broadcast_multiply_fusion.2
  640.0 1.5 broadcast_multiply_fusion
  (101 shorter events, 3.6 us)
Async XLA Ops:
  7.2 50.6 %copy-start = (bf16[512,1536]{1,0:T(8,128)(2,1)S(1)}, bf16[512,1536]{1,0:T(8,128)(2,1)}, u32[]{:S(2)}) copy-start(bf16[512,1536]{1,0:T(8,128)(2,1)} %param.29) | copy-start | bytes 4718596
  7.2 5.4 copy-start.2
  12.6 21.9 %copy-start.13 = (f32[128,512]{1,0:T(8,128)S(1)}, f32[128,512]{1,0:T(8,128)}, u32[]{:S(2)}) copy-start(f32[128,512]{1,0:T(8,128)} %param.27) | copy-start | bytes 786436
  12.6 21.9 %copy-start.17 = (s32[512]{0:T(512)S(1)}, s32[512]{0:T(512)}, u32[]{:S(2)}) copy-start(s32[512]{0:T(512)} %param.20) | copy-start | bytes 6148
  12.6 22.5 %copy-start.19 = (bf16[512,128]{1,0:T(8,128)(2,1)S(1)}, bf16[512,128]{1,0:T(8,128)(2,1)}, u32[]{:S(2)}) copy-start(bf16[512,128]{1,0:T(8,128)(2,1)} %param.22) | copy-start | bytes 393220
  12.6 22.5 %copy-start.20 = (bf16[128,512]{1,0:T(8,128)(2,1)S(1)}, bf16[128,512]{1,0:T(8,128)(2,1)}, u32[]{:S(2)}) copy-start(bf16[128,512]{1,0:T(8,128)(2,1)} %param.26) | copy-start | bytes 393220
  22.8 24.6 %all-to-all-start = ((s32[128,1,12]{2,1,0:T(1,128)}), s32[128,1,12]{2,1,0:T(1,128)S(1)}, u32[]{:S(2)}, u32[]{:S(2)}) async-start(s32[128,1,12]{2,1,0:T(1,128)} %bitcast.6), calls=%async_computation | async-start | bytes 131072 | tf_op jit(solution)/shard_map/all_to_all | solution.py:129
  44.7 13.1 %copy-start.10 = (bf16[256,512]{1,0:T(8,128)(2,1)S(1)}, bf16[256,512]{1,0:T(8,128)(2,1)}, u32[]{:S(2)}) copy-start(bf16[256,512]{1,0:T(8,128)(2,1)} %param.25) | copy-start | bytes 786436
  47.5 40.1 %all-to-all-start.1 = ((bf16[128,12,512]{2,1,0:T(8,128)(2,1)}), bf16[128,12,512]{2,1,0:T(8,128)(2,1)}, u32[]{:S(2)}, u32[]{:S(2)}) async-start(bf16[128,12,512]{2,1,0:T(8,128)(2,1)} %broadcast_select_fusion), calls=%async_computation.1 | async-start | bytes 4194304 | tf_op jit(solution)/shard_map/all_to_all | solution.py:130
  57.7 45.0 %copy-start.21 = (f32[1536]{0:T(1024)S(1)}, f32[1536]{0:T(1024)}, u32[]{:S(2)}) copy-start(f32[1536]{0:T(1024)} %param.30) | copy-start | bytes 18436
  57.7 170.3 %all-gather.2.cloned.1.call-start = ((), (), s32[]{:S(2)}) async-start(), calls=%async_computation.3 | async-start | bytes 33816576 | tf_op jit(solution)/shard_map/all_gather | solution.py:155
  112.0 7.5 %copy-start.4 = (bf16[512,512]{1,0:T(8,128)(2,1)S(1)}, bf16[512,512]{1,0:T(8,128)(2,1)}, u32[]{:S(2)}) copy-start(bf16[512,512]{1,0:T(8,128)(2,1)} %param.24) | copy-start | bytes 1572868
  112.0 7.5 %copy-start.6 = (bf16[512,512]{1,0:T(8,128)(2,1)S(1)}, bf16[512,512]{1,0:T(8,128)(2,1)}, u32[]{:S(2)}) copy-start(bf16[512,512]{1,0:T(8,128)(2,1)} %param.35) | copy-start | bytes 1572868
  112.0 8.0 %copy-start.14 = (s32[512,10]{0,1:T(8,128)S(1)}, s32[512,10]{0,1:T(8,128)}, u32[]{:S(2)}) copy-start(s32[512,10]{0,1:T(8,128)} %param.19) | copy-start | bytes 61444
  112.0 8.3 %copy-start.15 = (s32[512,10]{0,1:T(8,128)S(1)}, s32[512,10]{0,1:T(8,128)}, u32[]{:S(2)}) copy-start(s32[512,10]{0,1:T(8,128)} %param.21) | copy-start | bytes 61444
  113.6 7.1 %copy-start.16 = (f32[512,10]{0,1:T(8,128)S(1)}, f32[512,10]{0,1:T(8,128)}, u32[]{:S(2)}) copy-start(f32[512,10]{0,1:T(8,128)} %param.23) | copy-start | bytes 61444
  113.6 37.4 %all-to-all-start.2 = ((bf16[128,12,512]{2,1,0:T(8,128)(2,1)}), bf16[128,12,512]{2,1,0:T(8,128)(2,1)}, u32[]{:S(2)}, u32[]{:S(2)}) async-start(bf16[128,12,512]{2,1,0:T(8,128)(2,1)} %reshape.156), calls=%async_computation.2 | async-start | bytes 4194304 | tf_op jit(solution)/shard_map/all_to_all | solution.py:146
  119.4 517.3 %all-reduce.4.cloned.1.call-start = ((), (), s32[]{:S(2)}) async-start(), calls=%async_computation.4 | async-start | bytes 8388608 | tf_op jit(solution)/shard_map/psum | solution.py:173
  157.5 153.9 %copy-start.18 = (bf16[512,512]{1,0:T(8,128)(2,1)S(1)}, bf16[512,512]{1,0:T(8,128)(2,1)}, u32[]{:S(2)}) copy-start(bf16[512,512]{1,0:T(8,128)(2,1)} %param.34) | copy-start | bytes 1572868
  318.5 8.4 %copy-start.11 = (bf16[512,512]{1,0:T(8,128)(2,1)S(1)}, bf16[512,512]{1,0:T(8,128)(2,1)}, u32[]{:S(2)}) copy-start(bf16[512,512]{1,0:T(8,128)(2,1)} %param.33) | copy-start | bytes 1572868
  326.9 4.9 copy-start.12
  346.9 61.2 %slice-start.4 = ((s8[5242880]{0:T(1024)(128)(4,1)}), s8[4194304]{0:T(1024)(128)(4,1)S(1)}, s32[]{:S(2)}) async-start(s8[5242880]{0:T(1024)(128)(4,1)} %bitcast.78), calls=%async_computation.9 | async-start | bytes 8388608
  356.7 51.4 %slice-start.5 = ((s8[5242880]{0:T(1024)(128)(4,1)}), s8[1048576]{0:T(1024)(128)(4,1)S(1)}, s32[]{:S(2)}) async-start(s8[5242880]{0:T(1024)(128)(4,1)} %bitcast.78), calls=%async_computation.10 | async-start | bytes 2097152
  425.5 9.1 %slice-start = ((s8[5242880]{0:T(1024)(128)(4,1)}), s8[4194304]{0:T(1024)(128)(4,1)S(1)}, s32[]{:S(2)}) async-start(s8[5242880]{0:T(1024)(128)(4,1)} %bitcast.74), calls=%async_computation.5 | async-start | bytes 8388608
  433.7 1.2 slice-start.1
  446.9 4.6 copy-start.5
  450.8 2.5 copy-start.3
  462.4 14.8 %slice-start.6 = ((s8[5242880]{0:T(1024)(128)(4,1)}), s8[1048576]{0:T(1024)(128)(4,1)S(1)}, s32[]{:S(2)}) async-start(s8[5242880]{0:T(1024)(128)(4,1)} %bitcast.80), calls=%async_computation.11 | async-start | bytes 2097152
  471.1 6.1 slice-start.7
  475.6 2.6 slice-start.2
  477.2 1.6 slice-start.3
  482.6 1.0 copy-start.7
  636.7 3.3 copy-start.8
  636.7 3.3 copy-start.9
  636.7 4.8 copy-start.1
Sparse Core Ops, SparseCore 0:
  106.1 121.8 all-gather.1
  482.7 153.9 all-reduce.3
where the time goes:
time: 659 us; the launch traced here: 649 us
  waiting for transfers between devices  269 us (41%)
  local copies, waits for them, and re-layouts  163 us (25%)
  other arithmetic  130 us (20%)
  matrix products  44.2 us (7%)
  starting transfers between devices  27.6 us (4%)
  between operations  15.2 us (2%)
    psum x1, waiting for transfers between devices, shards(): lax.psum((grad_q.astype(jnp.float32), grad_k.astype(jnp.float32), grad_v....  152 us
    gather x1, local copies, waits for them, and re-layouts, shards(): nearby = whole_table[entries].reshape(events, fanout, columns)  83.5 us
    all_gather x1, waiting for transfers between devices, shards(): whole_table = lax.all_gather(new_memory, 'node', axis=0, tiled=True)  70.5 us
    sub x1, other arithmetic, attend(): probs = jax.nn.softmax(scores, axis=-1).astype(jnp.bfloat16)  51.3 us
    all_to_all x1, waiting for transfers between devices, shards(): lax.all_to_all(padded[flat_in].reshape(devices, cap_message, columns), 'n...  29.6 us
    all_to_all x1, waiting for transfers between devices, shards(): lax.all_to_all(outgoing, 'node', split_axis=0, concat_axis=0, tiled=True)  16.6 us
  transfers between devices with their start and end apart: 5, of which 4 were waited for; matrix products, arithmetic and copies ran while one was open for 7% of the time, Pallas kernels for 0%

commit v1 on v0

v1 whole, which is shorter than its diff:
```python
import math

import jax
import jax.numpy as jnp
from jax import lax
from jax.experimental import pallas as pl
from jax.experimental.pallas import tpu as pltpu
from jax.sharding import PartitionSpec as P

HEADS = 2
CAP = 12
SLOTS = 16
BLOCK = 64
UNROLL = 16

F32 = jnp.float32
BF16 = jnp.bfloat16


def dot(a, b):
    return jnp.dot(a, b, preferred_element_type=F32)


def dot_tn(a, b):
    return lax.dot_general(a, b, (((0,), (0,)), ((), ())), preferred_element_type=F32)


def dot_nt(a, b):
    return lax.dot_general(a, b, (((1,), (1,)), ((), ())), preferred_element_type=F32)


def flag(condition):
    return jnp.where(condition, 1.0, 0.0).astype(BF16)


def iota(shape, axis):
    return lax.broadcasted_iota(jnp.int32, shape, axis)


def sigmoid(v):
    return 1.0 / (1.0 + jnp.exp(-v))


def split_table(table):
    high = table.astype(BF16)
    low = (table - high.astype(F32)).astype(BF16)
    return jnp.concatenate([high, low], axis=0)


def pack_body(node_rows, devices, node_ref, bucket_ref, feature_ref, out_ref):
    nodes = node_ref[...]
    events = nodes.shape[1]
    owner = nodes // node_rows
    local = nodes - owner * node_rows
    marked = iota((devices, events), 0) == owner
    marks = flag(marked)
    before = flag(iota((events, events), 0) < iota((events, events), 1))
    earlier = dot(marks, before)
    rank = jnp.sum(jnp.where(marked, earlier, 0.0), axis=0, keepdims=True).astype(jnp.int32)
    lane = iota((128, events), 0)
    named = jnp.where(lane == rank, local + 1, 0) + jnp.where(
        lane == rank + SLOTS, bucket_ref[...], 0
    )
    meta = dot_nt(marks, named.astype(F32).astype(BF16)).astype(BF16)
    slots = devices * SLOTS
    place = flag(iota((slots, events), 0) == owner * SLOTS + rank)
    spots = flag(iota((slots, devices), 0) == iota((slots, devices), 1) * SLOTS + CAP)
    out_ref[...] = (dot(place, feature_ref[...]) + dot(spots, meta)).astype(BF16)


def memory_body(
    arrived_ref,
    memory_ref,
    edge_ref,
    time_ref,
    input_ref,
    hidden_ref,
    bias_ref,
    out_ref,
    rows_ref,
):
    rows_ref[...] = arrived_ref[...].astype(F32)
    sources = rows_ref.shape[0] // SLOTS
    node_rows, columns = memory_ref.shape
    previous = memory_ref[...]
    meta = rows_ref[pl.ds(CAP, sources, stride=SLOTS), :].astype(jnp.int32)
    table = split_table(time_ref[...])
    buckets = time_ref.shape[0]
    totals = jnp.zeros((node_rows, columns), F32)
    counts = jnp.zeros((node_rows, 128), F32)
    ones = jnp.ones((sources, 128), BF16)
    for r in range(CAP):
        feature = rows_ref[pl.ds(r, sources, stride=SLOTS), :].astype(BF16)
        bucket = flag(iota((sources, buckets), 1) == meta[:, SLOTS + r : SLOTS + r + 1])
        before = dot(feature, edge_ref[...]) + dot(
            jnp.concatenate([bucket, bucket], axis=1), table
        )
        message = (before / (1.0 + jnp.exp(-before))).astype(BF16)
        chosen = flag(iota((sources, node_rows), 1) + 1 == meta[:, r : r + 1])
        totals += dot_tn(chosen, message)
        counts += dot_tn(chosen, ones)
    count = counts[:, :1]
    aggregate = (totals / jnp.maximum(count, 1.0)).astype(BF16)
    inputs = dot(aggregate, input_ref[...]) + bias_ref[...]
    hidden = dot(previous, hidden_ref[...])
    update = sigmoid(inputs[:, :columns] + hidden[:, :columns])
    resets = sigmoid(inputs[:, columns : 2 * columns] + hidden[:, columns : 2 * columns])
    candidate = jnp.tanh(inputs[:, 2 * columns :] + resets * hidden[:, 2 * columns :])
    kept = previous.astype(F32)
    updated = (1.0 - update) * candidate + update * kept
    out_ref[...] = jnp.where(count > 0, updated, kept).astype(BF16)


def attend_body(
    index_ref,
    table_hbm,
    bucket_ref,
    affinity_ref,
    upstream_ref,
    time_ref,
    query_ref,
    both_ref,
    mix_ref,
    embedding_ref,
    grads_ref,
    table_ref,
    rows_ref,
    keys_ref,
    values_ref,
    change_ref,
    sums_ref,
    both_sums_ref,
    sem,
):
    step = pl.program_id(0)
    steps = pl.num_programs(0)
    block, fanout = bucket_ref.shape
    columns = query_ref.shape[0]
    head = columns // HEADS
    near = block * fanout
    picked = near + block
    pieces = columns // 128

    @pl.when(step == 0)
    def _():
        copy = pltpu.make_async_copy(table_hbm, table_ref, sem)
        copy.start()
        sums_ref[...] = jnp.zeros_like(sums_ref)
        both_sums_ref[...] = jnp.zeros_like(both_sums_ref)
        copy.wait()

    def fetch(i, carry):
        for u in range(UNROLL):
            row = i * UNROLL + u
            node = index_ref[step * picked + row]
            rows_ref[pl.ds(row * pieces, pieces), :] = table_ref[node].astype(F32)
        return carry

    lax.fori_loop(0, picked // UNROLL, fetch, 0)

    gathered = jnp.concatenate(
        [
            rows_ref[pl.ds(c, picked, stride=pieces), :].astype(BF16)
            for c in range(pieces)
        ],
        axis=1,
    )
    nearby = gathered[:near]
    target = gathered[near:]
    buckets = time_ref.shape[0] // 2
    lane = iota((block, buckets), 1)
    marks = jnp.concatenate(
        [flag(lane == bucket_ref[:, j : j + 1]) for j in range(fanout)], axis=0
    )
    keys_ref[...] = (
        dot(nearby, both_ref[:, :columns])
        + dot(jnp.concatenate([marks, marks], axis=1), time_ref[...])
    ).astype(BF16)
    values_ref[...] = dot(nearby, both_ref[:, columns:]).astype(BF16)
    query_half = dot(target, query_ref[...]).astype(BF16)
    upstream = upstream_ref[...]
    pull_half = dot_nt(upstream, mix_ref[...]).astype(BF16)
    query = query_half.astype(F32)
    pull = pull_half.astype(F32)
    scale = 1.0 / math.sqrt(head)
    mixed = []
    query_pull = []
    for h in range(HEADS):
        cols = slice(h * head, (h + 1) * head)
        q = query[:, cols]
        g = pull[:, cols]
        scores = []
        slopes = []
        for j in range(fanout):
            part = pl.ds(j * block, block)
            key = keys_ref[part, cols].astype(F32)
            value = values_ref[part, cols].astype(F32)
            score = jnp.sum(q * key, axis=1, keepdims=True) * scale
            scores.append(score + affinity_ref[:, j : j + 1])
            slope = jnp.sum(g * value, axis=1, keepdims=True)
            slopes.append(slope.astype(BF16).astype(F32))
        top = scores[0]
        for j in range(1, fanout):
            top = jnp.maximum(top, scores[j])
        powers = [jnp.exp(s - top) for s in scores]
        total = powers[0]
        for j in range(1, fanout):
            total = total + powers[j]
        over = 1.0 / total
        probs = [p * over for p in powers]
        mean = probs[0] * slopes[0]
        for j in range(1, fanout):
            mean = mean + probs[j] * slopes[j]
        mix = jnp.zeros((block, head), F32)
        back = jnp.zeros((block, head), F32)
        for j in range(fanout):
            part = pl.ds(j * block, block)
            key = keys_ref[part, cols].astype(F32)
            value = values_ref[part, cols].astype(F32)
            prob = probs[j].astype(BF16).astype(F32)
            turn = probs[j] * (slopes[j] - mean) * scale
            mix = mix + prob * value
            back = back + turn * key
            change_ref[part, cols] = (turn * q).astype(BF16)
            change_ref[part, pl.ds(columns + h * head, head)] = (prob * g).astype(BF16)
        mixed.append(mix.astype(BF16))
        query_pull.append(back.astype(BF16))
    mixed = jnp.concatenate(mixed, axis=1)
    query_pull = jnp.concatenate(query_pull, axis=1)
    embedding_ref[...] = (dot(mixed, mix_ref[...]) + target.astype(F32)).astype(BF16)
    sums_ref[:, :columns] += dot_tn(target, query_pull)
    sums_ref[:, columns:] += dot_tn(mixed, upstream)
    both_sums_ref[...] += dot_tn(nearby, change_ref[...])

    @pl.when(step == steps - 1)
    def _():
        grads_ref[pl.ds(0, columns), :] = sums_ref[:, :columns].astype(BF16)
        grads_ref[pl.ds(columns, columns), :] = both_sums_ref[:, :columns].astype(BF16)
        grads_ref[pl.ds(2 * columns, columns), :] = both_sums_ref[:, columns:].astype(BF16)
        grads_ref[pl.ds(3 * columns, columns), :] = sums_ref[:, columns:].astype(BF16)


def attend(table, index, buckets, affinity, upstream, time_pair, query_weight, both, mix_weight):
    events, fanout = buckets.shape
    columns = query_weight.shape[0]
    picked = BLOCK * (fanout + 1)
    pieces = columns // 128
    whole = lambda shape: pl.BlockSpec(shape, lambda i, *_: (0,) * len(shape))
    rows = lambda width: pl.BlockSpec((BLOCK, width), lambda i, *_: (i, 0))
    spec = pltpu.PrefetchScalarGridSpec(
        num_scalar_prefetch=1,
        grid=(events // BLOCK,),
        in_specs=[
            pl.BlockSpec(memory_space=pl.ANY),
            rows(fanout),
            rows(fanout),
            rows(columns),
            whole(time_pair.shape),
            whole(query_weight.shape),
            whole(both.shape),
            whole(mix_weight.shape),
        ],
        out_specs=[rows(columns), whole((4 * columns, columns))],
        scratch_shapes=[
            pltpu.VMEM(table.shape, BF16),
            pltpu.VMEM((picked * pieces, 128), F32),
            pltpu.VMEM((BLOCK * fanout, columns), BF16),
            pltpu.VMEM((BLOCK * fanout, columns), BF16),
            pltpu.VMEM((BLOCK * fanout, 2 * columns), BF16),
            pltpu.VMEM((columns, 2 * columns), F32),
            pltpu.VMEM((columns, 2 * columns), F32),
            pltpu.SemaphoreType.DMA,
        ],
    )
    return pl.pallas_call(
        attend_body,
        grid_spec=spec,
        out_shape=[
            jax.ShapeDtypeStruct((events, columns), BF16),
            jax.ShapeDtypeStruct((4 * columns, columns), BF16),
        ],
        compiler_params=pltpu.CompilerParams(
            dimension_semantics=("arbitrary",), vmem_limit_bytes=58 << 20
        ),
        name="attend",
    )(index, table, buckets, affinity, upstream, time_pair, query_weight, both, mix_weight)


def shards(
    event_node,
    neighbours,
    event_bucket,
    neighbour_bucket,
    edge_features,
    affinity,
    upstream,
    node_memory,
    edge_weight,
    time_message,
    input_weight,
    hidden_weight,
    gate_bias,
    time_key,
    query_weight,
    key_weight,
    value_weight,
    out_weight,
):
    devices = lax.axis_size("node")
    node_rows, columns = node_memory.shape
    events, fanout = neighbours.shape
    width = edge_features.shape[1]

    packed = pl.pallas_call(
        lambda *refs: pack_body(node_rows, devices, *refs),
        out_shape=jax.ShapeDtypeStruct((devices * SLOTS, width), BF16),
        name="pack",
    )(event_node.reshape(1, events), event_bucket.reshape(1, events), edge_features)
    arrived = lax.all_to_all(
        packed.reshape(devices, SLOTS, width), "node", split_axis=0, concat_axis=0, tiled=True
    )
    new_memory = pl.pallas_call(
        memory_body,
        out_shape=jax.ShapeDtypeStruct((node_rows, columns), BF16),
        scratch_shapes=[pltpu.VMEM((devices * SLOTS, width), F32)],
        name="memory",
    )(
        arrived.reshape(devices * SLOTS, width),
        node_memory,
        edge_weight,
        time_message,
        input_weight,
        hidden_weight,
        gate_bias.reshape(1, -1),
    )
    table = lax.all_gather(
        new_memory.reshape(node_rows, columns // 128, 128), "node", axis=0, tiled=True
    )
    steps = events // BLOCK
    index = jnp.concatenate(
        [
            neighbours.reshape(steps, BLOCK, fanout).transpose(0, 2, 1).reshape(steps, -1),
            event_node.reshape(steps, BLOCK),
        ],
        axis=1,
    ).reshape(-1)
    embedding, grads = attend(
        table,
        index,
        neighbour_bucket,
        affinity,
        upstream,
        split_table(time_key),
        query_weight,
        jnp.concatenate([key_weight, value_weight], axis=1),
        out_weight,
    )
    share = 4 * columns // devices
    parts = lax.all_to_all(
        grads.reshape(devices, share, columns), "node", split_axis=0, concat_axis=0, tiled=True
    )
    factor = 1.0 / math.sqrt(events * devices)
    own = (jnp.sum(parts.astype(F32), axis=0) * factor).astype(BF16)
    spread = lax.all_to_all(
        jnp.broadcast_to(own[None], (devices, share, columns)),
        "node",
        split_axis=0,
        concat_axis=0,
        tiled=True,
    )
    total = spread.reshape(4, columns, columns).astype(F32)
    return (embedding, new_memory, total[0], total[1], total[2], total[3])


def solution(mesh):
    placed = (
        P("node"),
        P("node", None),
        P("node"),
        P("node", None),
        P("node", None),
        P("node", None),
        P("node", None),
        P("node", None),
    ) + (P(),) * 10
    return jax.shard_map(
        shards,
        mesh=mesh,
        in_specs=placed,
        out_specs=(P("node", None), P("node", None), P(), P(), P(), P()),
        check_vma=False,
    )
```

time: 659 us -> 291 us (0.44); the launches traced: 649 us -> 290 us
  waiting for transfers between devices: 269 us -> 111 us
  local copies, waits for them, and re-layouts: 163 us -> 9.05 us
  other arithmetic: 130 us -> 2.25 us
  blocking collectives: 0 us -> 72 us
  Pallas kernels: 0 us -> 70.1 us
  matrix products: 44.2 us -> 0 us
  starting transfers between devices: 27.6 us -> 11.5 us
    psum x1 -> x0, waiting for transfers between devices: 152 us -> none  [shards(): lax.psum((grad_q.astype(jnp.float32), grad_k.astype(jnp.float32), grad_v....]
    gather x6 -> x0, local copies, waits for them, and re-layouts: 109 us -> none  [the longest x1 83.5 us: shards(): nearby = whole_table[entries].reshape(events, fanout, columns)]
    all_to_all x0 -> x2, blocking collectives: none -> 72 us  [the longest x1 37.4 us: shards(): lax.all_to_all(grads.reshape(devices, share, columns), 'node', split_axis...]
    pallas_call x0 -> x3, Pallas kernels: none -> 70.1 us  [the longest x1 58.7 us: attend(): pl.pallas_call(attend_body, grid_spec=spec, out_shape=[jax.ShapeDtypeStru...]
    sub x1 -> x0, other arithmetic: 51.3 us -> none  [attend(): probs = jax.nn.softmax(scores, axis=-1).astype(jnp.bfloat16)]
    dot_general x16 -> x0, matrix products: 44.2 us -> none  [the longest x2 10.9 us: attend(): jnp.dot(flat_rows, value_weight, preferred_element_type=jnp.float32)]
    all_to_all x3 -> x1, waiting for transfers between devices: 46.2 us -> 12.1 us  [shards(): lax.all_to_all(packed.reshape(devices, SLOTS, width), 'node', split_axis=...]
    all_gather x1, waiting for transfers between devices: 70.5 us -> 98.8 us  [shards(): lax.all_gather(new_memory.reshape(node_rows, columns // 128, 128), 'node'...]
  transfers between devices with their start and end apart: 5 -> 2, of which waited for: 4 -> 2; matrix products, arithmetic and copies ran while one was open for 7% -> 2% of each run, Pallas kernels for 0% -> 0%
where the time goes in v1:
time: 291 us; the launch traced here: 290 us
  waiting for transfers between devices  111 us (38%)
  blocking collectives  72 us (25%)
  Pallas kernels  70.1 us (24%)
  between operations  14.1 us (5%)
  starting transfers between devices  11.5 us (4%)
  local copies, waits for them, and re-layouts  9.05 us (3%)
    all_gather x1, waiting for transfers between devices, shards(): lax.all_gather(new_memory.reshape(node_rows, columns // 128, 128), 'node'...  98.8 us
    pallas_call x1, Pallas kernels, attend(): pl.pallas_call(attend_body, grid_spec=spec, out_shape=[jax.ShapeDtypeStru...  58.7 us
    all_to_all x1, blocking collectives, shards(): lax.all_to_all(grads.reshape(devices, share, columns), 'node', split_axis...  37.4 us
    all_to_all x1, blocking collectives, shards(): lax.all_to_all(jnp.broadcast_to(own[None], (devices, share, columns)), 'n...  34.6 us
    all_to_all x1, waiting for transfers between devices, shards(): lax.all_to_all(packed.reshape(devices, SLOTS, width), 'node', split_axis=...  12.1 us
    all_to_all x1, starting transfers between devices, shards(): lax.all_to_all(packed.reshape(devices, SLOTS, width), 'node', split_axis=...  11.5 us
    pallas_call x1, Pallas kernels, shards(): pl.pallas_call(memory_body, out_shape=jax.ShapeDtypeStruct((node_rows, co...  8.28 us
  transfers between devices with their start and end apart: 2, of which 2 were waited for; matrix products, arithmetic and copies ran while one was open for 2% of the time, Pallas kernels for 0%

profile of v1, /device:TPU:1, one launch (start us, length us, event | category | flops | bytes accessed | tf_op | source)
XLA Modules:
  0.0 290.0 jit_solution(10564098311622104330)
XLA Ops:
  7.2 3.1 %pack.1 = bf16[2048,128]{1,0:T(8,128)(2,1)} custom-call(s32[1,512]{1,0:T(1,128)} %bitcast.22, s32[1,512]{1,0:T(1,128)} %bitcast.23, bf16[512,128]{1,0:T(8,128)(2,1)} %refs_2_.1), custom_call_target="tpu_custom_call" | custom-call | tf_op jit(solution)/shard_map/pack/pallas_call | solution.py:314
  10.3 11.5 %all-to-all-start = ((bf16[128,16,128]{2,1,0:T(8,128)(2,1)}), bf16[128,16,128]{2,1,0:T(8,128)(2,1)S(1)}, u32[]{:S(2)}, u32[]{:S(2)}) async-start(bf16[128,16,128]{2,1,0:T(8,128)(2,1)} %bitcast.15), calls=%async_computation | async-start | bytes 1048576 | tf_op jit(solution)/shard_map/all_to_all | solution.py:319
  21.8 0.0 all-gather.2.cloned.1.call-start
  21.8 1.3 reshape.67.bias_ref
  23.1 12.1 %all-to-all-done = bf16[128,16,128]{2,1,0:T(8,128)(2,1)S(1)} async-done(((bf16[128,16,128]{2,1,0:T(8,128)(2,1)}), bf16[128,16,128]{2,1,0:T(8,128)(2,1)S(1)}, u32[]{:S(2)}, u32[]{:S(2)}) %all-to-all-start) | async-done | bytes 524320 | tf_op jit(solution)/shard_map/all_to_all | solution.py:319
  35.2 0.0 copy-start
  35.2 0.8 copy-done
  36.0 0.0 copy-start.7
  36.0 0.0 copy-start.6
  36.0 0.0 copy-start.4
  36.0 0.0 copy-start.5
  36.0 0.0 copy-start.3
  36.1 8.3 %memory.1 = bf16[256,512]{1,0:T(8,128)(2,1)} custom-call(bf16[2048,128]{1,0:T(8,128)(2,1)} %bitcast.14, bf16[256,512]{1,0:T(8,128)(2,1)} %memory_ref.1, bf16[128,512]{1,0:T(8,128)(2,1)} %edge_ref.1, f32[128,512]{1,0:T(8,128)} %time_ref.1, bf16[512,1536]{1,0:T(8,128)(2,1)} %input_ref.1, bf16[512,1536]{1,0:T(8,128)(2,1)} %hidden_ref.1, f32[1,1536]{1,0:T(1,128)} %reshape.67.bias_ref), custom_call_target="tpu_custom_call" | custom-call | tf_op jit(solution)/shard_map/memory/pallas_call | solution.py:322
  44.3 0.0 copy-start.1
  44.3 0.0 copy-start.2
  44.3 1.8 reshape.68
  46.1 0.0 all-gather.2.cloned.1.call-update
  46.2 0.0 copy-done.7
  46.2 0.1 reshape.61
  46.3 0.0 copy-done.6
  46.3 0.1 reshape.59
  46.4 0.1 reshape.60
  46.4 0.7 reshape.62.index_ref
  47.1 0.0 copy-done.4
  47.1 0.9 copy.30.bucket_ref
  48.0 0.0 copy-done.5
  48.0 0.9 copy.31.affinity_ref
  48.8 0.0 copy-done.3
  48.9 0.7 pad_maximum_fusion.1.time_ref
  49.6 0.0 copy-done.1
  49.6 0.0 copy-done.2
  49.6 1.1 pad_maximum_fusion.both_ref
  50.7 98.8 %all-gather.2.cloned.1.call-done.table_hbm = bf16[32768,4,128]{2,1,0:T(4,128)(2,1)} async-done(((bf16[256,4,128]{2,1,0:T(4,128)(2,1)}), bf16[32768,4,128]{2,1,0:T(4,128)(2,1)}) %all-gather.2.cloned.1.call-update) | async-done | bytes 33554448 | tf_op jit(solution)/shard_map/all_gather | solution.py:336
  149.5 58.7 %attend.1 = (bf16[512,512]{1,0:T(8,128)(2,1)}, bf16[2048,512]{1,0:T(8,128)(2,1)}) custom-call(s32[5632]{0:T(1024)} %reshape.62.index_ref, bf16[32768,4,128]{2,1,0:T(4,128)(2,1)} %all-gather.2.cloned.1.call-done.table_hbm, s32[512,10]{1,0:T(8,128)} %copy.30.bucket_ref, f32[512,10]{1,0:T(8,128)} %copy.31.affinity_ref, bf16[512,512]{1,0:T(8,128)(2,1)} %upstream_ref.1, ...), custom_call_target="tpu_custom_call" | custom-call | tf_op jit(solution)/shard_map/attend/pallas_call | solution.py:275
  208.2 37.4 %all_to_all.15 = bf16[128,16,512]{2,1,0:T(8,128)(2,1)S(1)} all-to-all(bf16[128,16,512]{2,1,0:T(8,128)(2,1)} %bitcast.16), channel_id=1, replica_groups=mesh['node'=128] {'node'}, dimensions={0} | all-to-all | bytes 4194304 | tf_op jit(solution)/shard_map/all_to_all | solution.py:359
  245.7 0.4 convert_reduce_fusion
  246.1 0.3 broadcast_in_dim.2
  246.3 34.6 %all_to_all.16 = bf16[128,16,512]{2,1,0:T(8,128)(2,1)S(1)} all-to-all(bf16[128,16,512]{2,1,0:T(8,128)(2,1)S(1)} %broadcast_in_dim.2), channel_id=1, replica_groups=mesh['node'=128] {'node'}, dimensions={0} | all-to-all | bytes 4194304 | tf_op jit(solution)/shard_map/all_to_all | solution.py:364
  280.9 2.3 fusion
  (4 shorter events, 0.1 us)
Async XLA Ops:
  10.3 25.0 %all-to-all-start = ((bf16[128,16,128]{2,1,0:T(8,128)(2,1)}), bf16[128,16,128]{2,1,0:T(8,128)(2,1)S(1)}, u32[]{:S(2)}, u32[]{:S(2)}) async-start(bf16[128,16,128]{2,1,0:T(8,128)(2,1)} %bitcast.15), calls=%async_computation | async-start | bytes 1048576 | tf_op jit(solution)/shard_map/all_to_all | solution.py:319
  21.8 127.8 %all-gather.2.cloned.1.call-start = ((), (), s32[]{:S(2)}) async-start(), calls=%async_computation.3 | async-start | bytes 33816576 | tf_op jit(solution)/shard_map/all_gather | solution.py:336
  35.2 0.8 copy-start
  36.0 10.1 %copy-start.7 = (s32[512]{0:T(512)S(1)}, s32[512]{0:T(512)}, u32[]{:S(2)}) copy-start(s32[512]{0:T(512)} %param.18) | copy-start | bytes 6148
  36.0 10.2 %copy-start.6 = (s32[512,10]{0,1:T(8,128)S(1)}, s32[512,10]{0,1:T(8,128)}, u32[]{:S(2)}) copy-start(s32[512,10]{0,1:T(8,128)} %param.19) | copy-start | bytes 61444
  36.0 11.1 %copy-start.4 = (s32[512,10]{0,1:T(8,128)S(1)}, s32[512,10]{0,1:T(8,128)}, u32[]{:S(2)}) copy-start(s32[512,10]{0,1:T(8,128)} %param.21) | copy-start | bytes 61444
  36.0 11.9 %copy-start.5 = (f32[512,10]{0,1:T(8,128)S(1)}, f32[512,10]{0,1:T(8,128)}, u32[]{:S(2)}) copy-start(f32[512,10]{0,1:T(8,128)} %param.23) | copy-start | bytes 61444
  36.0 12.8 %copy-start.3 = (f32[128,512]{1,0:T(8,128)S(1)}, f32[128,512]{1,0:T(8,128)}, u32[]{:S(2)}) copy-start(f32[128,512]{1,0:T(8,128)} %param.31) | copy-start | bytes 786436
  44.3 5.2 %copy-start.1 = (bf16[512,512]{1,0:T(8,128)(2,1)S(1)}, bf16[512,512]{1,0:T(8,128)(2,1)}, u32[]{:S(2)}) copy-start(bf16[512,512]{1,0:T(8,128)(2,1)} %param.34) | copy-start | bytes 1572868
  44.3 5.2 %copy-start.2 = (bf16[512,512]{1,0:T(8,128)(2,1)S(1)}, bf16[512,512]{1,0:T(8,128)(2,1)}, u32[]{:S(2)}) copy-start(bf16[512,512]{1,0:T(8,128)(2,1)} %param.33) | copy-start | bytes 1572868
Sparse Core Ops, SparseCore 0:
  46.3 103.2 all-gather.1
